TPU v7x, 32 devices: a whole 2x2x4 slice. The times are simulated.
32 devices in a mesh: grp: 4 (over y, x), tp: 8 (over z, core).
Axes of the slice: x: 2, y: 2, z: 4, core: 2. Of those that a mesh axis runs over, the one named last changes fastest.
Arguments:
- key_cache: bfloat16 [4, 8, 768, 512], P('grp', 'tp'), may hold values from -6 to 6
- value_cache: bfloat16 [4, 8, 768, 512], P('grp', 'tp'), may hold values from -12 to 12
- lengths: int32 [4, 8], P('grp', 'tp'), may hold values from 256 to 768, as said below
- queries: bfloat16 [4, 1, 8, 8192], P('grp', None, 'tp'), may hold values from -12 to 12
- new_keys: bfloat16 [4, 1, 8, 512], P('grp', None, 'tp'), may hold values from -18 to 18
- new_values: bfloat16 [4, 1, 8, 512], P('grp', None, 'tp'), may hold values from -12 to 12
- residual: bfloat16 [4, 1, 8, 8192], P('grp', None, 'tp'), may hold values from -4 to 4
- norm_gain: float32 [8192], replicated, may hold values from 0.25 to 1.75
- gate_weight: bfloat16 [4, 13312, 8192], P('grp', 'tp'), may hold values from -0.0625 to 0.0625
- up_weight: bfloat16 [4, 13312, 8192], P('grp', 'tp'), may hold values from -0.0625 to 0.0625
- down_weight: bfloat16 [4, 13312, 8192], P('grp', 'tp'), may hold values from -0.0390625 to 0.0390625
Outputs:
- mixed: bfloat16 [4, 1, 8, 8192], P('grp', None, 'tp')
Inputs may be any that keep to these rules, and one draw needn't show every extreme that they name: `lengths`: some row has exactly 768 valid positions.
All inputs are finite; a program needn't handle non-finite values.
Results may differ from a plain program's by a relative error of at most 0.005.
Values may be sent and summed in bfloat16 or wider, within the bound.
A program may use at most 128 MiB of HBM per device.

v0:
```python
import functools

import jax
import jax.numpy as jnp
from jax import lax
from jax.experimental import pallas as pl
from jax.experimental.pallas import tpu as pltpu
from jax.sharding import PartitionSpec as P

HEADS = 64
HD = 128
KVH = 4
SHARE = HEADS // KVH

masked_score = -1e30
MESH_ID = pl.DeviceIdType.MESH
VMEM_BYTES = 66_000_000


def kernel(
    plan,
    lengths,
    queries,
    fresh_keys,
    fresh_values,
    residual,
    gain,
    key_hbm,
    value_hbm,
    gate_hbm,
    up_hbm,
    down_hbm,
    out,
    keys,
    values,
    hidden,
    normed,
    box,
    wide,
    rows,
    act,
    part,
    slots,
    down_slots,
    cache_sem,
    slot_sem,
    down_sem,
    send_sem,
    recv_sem,
):
    (half, members, chunk, chunks, ring, down_cols, down_chunks, down_ring, batch) = plan
    peers = half * members
    blocks = HEADS
    group = lax.axis_index("grp")
    member = lax.axis_index("tp")
    serving = group < half
    mine = lax.rem(group, half) * members + member
    other = jnp.where(serving, half, 0)
    barrier = pltpu.get_barrier_semaphore()

    def peer_id(i):
        return {"grp": other + i // members, "tp": lax.rem(i, members)}

    def slot_copies(i, s):
        start = pl.multiple_of(i * chunk, chunk)
        return (
            pltpu.make_async_copy(
                gate_hbm.at[0, pl.ds(start, chunk), :], slots.at[s, 0], slot_sem.at[s]
            ),
            pltpu.make_async_copy(
                up_hbm.at[0, pl.ds(start, chunk), :], slots.at[s, 1], slot_sem.at[s]
            ),
        )

    def down_copy(c, s):
        start = pl.multiple_of(c * down_cols, down_cols)
        return pltpu.make_async_copy(
            down_hbm.at[0, :, pl.ds(start, down_cols)], down_slots.at[s], down_sem.at[s]
        )

    key_copy = pltpu.make_async_copy(key_hbm.at[0, 0], keys, cache_sem.at[0])
    value_copy = pltpu.make_async_copy(value_hbm.at[0, 0], values, cache_sem.at[1])

    @pl.when(serving)
    def _():
        key_copy.start()
        value_copy.start()

    @pl.when(jnp.logical_not(serving))
    def _():
        for i in range(min(ring, chunks)):
            for copy in slot_copies(i, i):
                copy.start()

    @pl.loop(0, peers)
    def _(i):
        pl.semaphore_signal(barrier, inc=1, device_id=peer_id(i), device_id_type=MESH_ID)

    @pl.when(serving)
    def _():
        slot_count = keys.shape[0]
        scale = HD ** (-0.5)
        usable = lax.broadcasted_iota(jnp.int32, (SHARE, slot_count), 1) < lengths[0, 0]
        key_copy.wait()
        value_copy.wait()
        spread = jnp.zeros((1, 1), jnp.float32)
        for j in range(KVH):
            head = slice(j * SHARE, (j + 1) * SHARE)
            lanes = slice(j * HD, (j + 1) * HD)
            own = queries[head, :]
            scores = (
                lax.dot_general(
                    own, keys[:, lanes], (((1,), (1,)), ((), ())),
                    preferred_element_type=jnp.float32,
                )
                * scale
            )
            scores = jnp.where(usable, scores, masked_score)
            fresh = (
                jnp.sum(
                    own.astype(jnp.float32) * fresh_keys[j : j + 1, :].astype(jnp.float32),
                    axis=-1, keepdims=True,
                )
                * scale
            )
            ceiling = jnp.maximum(jnp.max(scores, axis=-1, keepdims=True), fresh)
            expo = jnp.where(usable, jnp.exp(scores - ceiling), 0.0)
            fresh_expo = jnp.exp(fresh - ceiling)
            denominator = jnp.sum(expo, axis=-1, keepdims=True) + fresh_expo
            total = jnp.dot(
                expo.astype(jnp.bfloat16), values[:, lanes], preferred_element_type=jnp.float32
            )
            total = total + fresh_expo.astype(jnp.bfloat16).astype(jnp.float32) * fresh_values[
                j : j + 1, :
            ].astype(jnp.float32)
            row = residual[head, :].astype(jnp.float32) + total / denominator
            hidden[head, :] = row
            squares = jnp.sum(row * row, axis=-1, keepdims=True)
            spread = spread + jnp.sum(squares, axis=0, keepdims=True)
        factor = lax.rsqrt(spread / (HEADS * HD) + 1e-05)
        normed[...] = (hidden[...] * factor * gain[...]).astype(jnp.bfloat16)
        pl.semaphore_wait(barrier, peers)

        @pl.loop(0, peers)
        def _(i):
            to = lax.rem(mine + i, peers)
            pltpu.make_async_remote_copy(
                src_ref=normed,
                dst_ref=box.at[mine],
                send_sem=send_sem,
                recv_sem=recv_sem,
                device_id=peer_id(to),
                device_id_type=MESH_ID,
            ).start()

        pltpu.make_async_copy(box, box, send_sem).wait()
        pltpu.make_async_copy(box, box, recv_sem).wait()

        for b in range(0, blocks, batch):
            band = slice(b, b + batch)
            total = hidden[band, :]
            feed = lax.fori_loop(
                0,
                peers,
                lambda f, so_far: so_far + box[f, band, :].astype(jnp.float32),
                jnp.zeros_like(total),
            )
            out[band, :] = (total + feed).astype(jnp.bfloat16)

    @pl.when(jnp.logical_not(serving))
    def _():
        out[...] = jnp.zeros_like(out)
        pl.semaphore_wait(barrier, peers)
        pltpu.make_async_copy(box, box, recv_sem).wait()
        for c in range(min(down_ring, down_chunks)):
            down_copy(c, c).start()

        @pl.loop(0, peers)
        def _(r):
            wide[pl.ds(pl.multiple_of(r * blocks, blocks), blocks), :] = box[r].astype(jnp.float32)

        for h in range(blocks):
            rows[:, h * HD : (h + 1) * HD] = wide[pl.ds(h, peers, stride=blocks), :].astype(
                jnp.bfloat16
            )

        numbers = (((1,), (1,)), ((), ()))

        def product(weights):
            mid = weights.shape[1] // 2
            return lax.dot_general(
                rows[:, :mid], weights[:, :mid], numbers, preferred_element_type=jnp.float32
            ) + lax.dot_general(
                rows[:, mid:], weights[:, mid:], numbers, preferred_element_type=jnp.float32
            )

        def hidden_units(i, s):
            pltpu.make_async_copy(slots.at[s], slots.at[s], slot_sem.at[s]).wait()
            gate = product(slots[s, 0])
            up = product(slots[s, 1])
            return (gate / (1.0 + jnp.exp(-gate)) * up).astype(jnp.bfloat16)

        if chunks == 1:
            act[...] = hidden_units(0, 0)
        else:

            @pl.loop(0, chunks)
            def _(i):
                s = lax.rem(i, ring)
                act[:, pl.ds(pl.multiple_of(i * chunk, chunk), chunk)] = hidden_units(i, s)

                @pl.when(i + ring < chunks)
                def _():
                    for copy in slot_copies(i + ring, s):
                        copy.start()

        per_chunk = down_cols // HD
        per_send = batch // per_chunk

        @pl.loop(0, down_chunks // per_send)
        def _(g):
            base = pl.multiple_of(g * batch, batch)
            for k in range(per_send):
                c = g * per_send + k
                s = lax.rem(c, down_ring)
                pltpu.make_async_copy(down_slots.at[s], down_slots.at[s], down_sem.at[s]).wait()
                feed = jnp.dot(act[...], down_slots[s], preferred_element_type=jnp.float32)

                @pl.when(c + down_ring < down_chunks)
                def _():
                    down_copy(c + down_ring, s).start()

                for h in range(per_chunk):
                    wide[pl.ds(base + k * per_chunk + h, peers, stride=blocks), :] = feed[
                        :, h * HD : (h + 1) * HD
                    ]

            @pl.loop(0, peers)
            def _(r):
                start = pl.multiple_of(r * blocks + base, batch)
                part[r, pl.ds(base, batch), :] = wide[pl.ds(start, batch), :].astype(jnp.bfloat16)

            @pl.loop(0, peers)
            def _(i):
                to = lax.rem(mine + i, peers)
                pltpu.make_async_remote_copy(
                    src_ref=part.at[to, pl.ds(base, batch), :],
                    dst_ref=box.at[mine, pl.ds(base, batch), :],
                    send_sem=send_sem,
                    recv_sem=recv_sem,
                    device_id=peer_id(to),
                    device_id_type=MESH_ID,
                ).start()

        pltpu.make_async_copy(part, part, send_sem).wait()


def local(
    key_cache,
    value_cache,
    lengths,
    queries,
    new_keys,
    new_values,
    residual,
    norm_gain,
    gate_weight,
    up_weight,
    down_weight,
):
    groups = lax.axis_size("grp")
    members = lax.axis_size("tp")
    half = groups // 2
    peers = half * members
    width = queries.shape[3]
    slot_count = key_cache.shape[2]
    units = gate_weight.shape[1]
    chunk = HD if units % HD == 0 else units
    chunks = units // chunk
    slot_bytes = 4 * chunk * width
    ring = max(1, min(chunks, 42_000_000 // slot_bytes))
    down_cols = 512
    down_chunks = width // down_cols
    down_ring = min(down_chunks, max(1, 14_000_000 // (2 * units * down_cols)))
    batch = 16
    plan = (half, members, chunk, chunks, ring, down_cols, down_chunks, down_ring, batch)
    vmem = pl.BlockSpec(memory_space=pltpu.VMEM)
    any_space = pl.BlockSpec(memory_space=pl.ANY)
    bf16 = jnp.bfloat16
    f32 = jnp.float32
    mixed = pl.pallas_call(
        functools.partial(kernel, plan),
        out_shape=jax.ShapeDtypeStruct((HEADS, HD), bf16),
        in_specs=[pl.BlockSpec(memory_space=pltpu.SMEM)] + [vmem] * 5 + [any_space] * 5,
        out_specs=vmem,
        scratch_shapes=[
            pltpu.VMEM((slot_count, KVH * HD), bf16),
            pltpu.VMEM((slot_count, KVH * HD), bf16),
            pltpu.VMEM((HEADS, HD), f32),
            pltpu.VMEM((HEADS, HD), bf16),
            pltpu.VMEM((peers, HEADS, HD), bf16),
            pltpu.VMEM((peers * HEADS, HD), f32),
            pltpu.VMEM((peers, width), bf16),
            pltpu.VMEM((peers, units), bf16),
            pltpu.VMEM((peers, HEADS, HD), bf16),
            pltpu.VMEM((ring, 2, chunk, width), bf16),
            pltpu.VMEM((down_ring, units, down_cols), bf16),
            pltpu.SemaphoreType.DMA((2,)),
            pltpu.SemaphoreType.DMA((ring,)),
            pltpu.SemaphoreType.DMA((down_ring,)),
            pltpu.SemaphoreType.DMA,
            pltpu.SemaphoreType.DMA,
        ],
        compiler_params=pltpu.CompilerParams(
            collective_id=0, has_side_effects=True, vmem_limit_bytes=VMEM_BYTES
        ),
    )(
        lengths,
        queries.reshape(HEADS, HD),
        new_keys.reshape(KVH, HD),
        new_values.reshape(KVH, HD),
        residual.reshape(HEADS, HD),
        norm_gain.reshape(HEADS, HD),
        key_cache,
        value_cache,
        gate_weight,
        up_weight,
        down_weight,
    )
    return mixed.reshape(1, 1, 1, width)


def solution(mesh):
    return jax.shard_map(
        local,
        mesh=mesh,
        in_specs=(
            P("grp", "tp", None, None),
            P("grp", "tp", None, None),
            P("grp", "tp"),
            P("grp", None, "tp", None),
            P("grp", None, "tp", None),
            P("grp", None, "tp", None),
            P("grp", None, "tp", None),
            P(),
            P("grp", "tp", None),
            P("grp", "tp", None),
            P("grp", "tp", None),
        ),
        out_specs=P("grp", None, "tp", None),
        check_vma=False,
    )
```

profile of v0, /device:TPU:0, one launch (start us, length us, event | category | flops | bytes accessed | tf_op | source)
XLA Modules:
  0.0 52.5 jit_solution(6571214720821019163)
XLA Ops:
  0.7 1.3 %reduce.1 = bf16[512]{0:T(512)(128)(2,1)} reduce(bf16[1,1,1,512]{3,2,1,0:T(2,128)(2,1)} %param.15, bf16[]{:T(256)} %constant.10), dimensions={0,1,2}, to_apply=%param.15.reduce_sub_computation | reduce | bytes 2050 | tf_op args[4]
  1.9 1.3 %reduce.2 = bf16[512]{0:T(512)(128)(2,1)} reduce(bf16[1,1,1,512]{3,2,1,0:T(2,128)(2,1)} %param.16, bf16[]{:T(256)} %constant.10), dimensions={0,1,2}, to_apply=%param.16.reduce_sub_computation | reduce | bytes 2050 | tf_op args[5]
  3.2 1.5 %reduce = bf16[8192]{0:T(1024)(128)(2,1)} reduce(bf16[1,1,1,8192]{3,2,1,0:T(2,128)(2,1)} %param.14, bf16[]{:T(256)} %constant.10), dimensions={0,1,2}, to_apply=%param.14.reduce_sub_computation | reduce | bytes 32770 | tf_op args[3]
  4.6 1.4 %reduce.3 = bf16[8192]{0:T(1024)(128)(2,1)} reduce(bf16[1,1,1,8192]{3,2,1,0:T(2,128)(2,1)} %param.17, bf16[]{:T(256)} %constant.10), dimensions={0,1,2}, to_apply=%param.17.reduce_sub_computation | reduce | bytes 32770 | tf_op args[6]
  6.1 45.1 %shard_map.109 = bf16[64,128]{1,0:T(8,128)(2,1)} custom-call(s32[1,1]{1,0:T(1,128)S(6)} %copy.12.lengths, bf16[64,128]{1,0:T(8,128)(2,1)} %bitcast.5, bf16[4,128]{1,0:T(4,128)(2,1)} %bitcast.8, bf16[4,128]{1,0:T(4,128)(2,1)} %bitcast.9, bf16[64,128]{1,0:T(8,128)(2,1)} %bitcast.6, f32[64,128]{1,0:T(8,128)} %bitcast.7, bf16[1,1,768,512]{3,2,1,0:T(8,128)(2,1)} %key_hbm.1, ...), custom_call_target="tpu_custom_call" | custom-call | tf_op jit(solution)/shard_map/pallas_call | solution.py:291
  51.2 1.3 %reshape.23 = bf16[1,1,1,8192]{3,2,1,0:T(2,128)(2,1)} reshape(bf16[64,128]{1,0:T(8,128)(2,1)} %shard_map.109) | data formatting | bytes 32768 | tf_op jit(solution)/shard_map/reshape | solution.py:330
where the time goes:
time: 53 us; the launch traced here: 52.5 us
  Pallas kernels  45.1 us (85%)
  other arithmetic  5.43 us (10%)
  local copies, waits for them, and re-layouts  1.34 us (3%)
  between operations  0.66 us (1%)
    pallas_call x1, Pallas kernels, local(): pl.pallas_call(functools.partial(kernel, plan), out_shape=jax.ShapeDtypeS...  45.1 us
    unnamed x4, other arithmetic  5.43 us
    reshape x1, local copies, waits for them, and re-layouts, local(): return mixed.reshape(1, 1, 1, width)  1.34 us

commit v1 on v0

v1 whole, which is shorter than its diff:
```python
import functools

import jax
import jax.numpy as jnp
from jax import lax
from jax.experimental import pallas as pl
from jax.experimental.pallas import tpu as pltpu
from jax.sharding import PartitionSpec as P

HEADS = 64
HD = 128
KVH = 4
SHARE = HEADS // KVH
CORES = 2
STRIDE = HEADS + 8

masked_score = -1e30
MESH_ID = pl.DeviceIdType.MESH
VMEM_BYTES = 67_000_000
NT = (((1,), (1,)), ((), ()))
f32 = jnp.float32
bf16 = jnp.bfloat16


def kernel(
    plan,
    lengths,
    gain_hbm,
    queries_hbm,
    fresh_keys_hbm,
    fresh_values_hbm,
    residual_hbm,
    key_hbm,
    value_hbm,
    gate_hbm,
    up_hbm,
    down_hbm,
    out,
    keys,
    values,
    queries,
    fresh_keys,
    fresh_values,
    residual,
    gain,
    hidden,
    normed,
    box,
    wide,
    rows,
    gate_out,
    up_out,
    act,
    keep,
    cross_out,
    cross_in,
    part,
    back,
    slots,
    down_slots,
    cache_sem,
    small_sem,
    slot_sem,
    down_sem,
    row_send,
    row_recv,
    pass_send,
    cross_send,
    cross_recv,
    back_send,
    back_recv,
):
    (half, members, chunk, chunks, ring, down_cols, down_chunks, down_ring, batch) = plan
    peers = half * members
    pairs = peers // CORES
    per_group = members // CORES
    group = lax.axis_index("grp")
    member = lax.axis_index("tp")
    serving = group < half
    core = lax.rem(member, CORES)
    place = member // CORES
    mine = lax.rem(group, half) * per_group + place
    other = jnp.where(serving, half, 0)
    barrier = pltpu.get_barrier_semaphore()
    batches = HEADS // batch
    per_batch = batch * HD // down_cols

    flip = 1 - 2 * (2 * place // per_group)

    def pair_at(i):
        off = per_group - 1 - i // half
        spot = lax.rem(place + off * flip + per_group, per_group)
        side = lax.rem(lax.rem(group, half) + half - 1 - lax.rem(i, half), half)
        return side * per_group + spot

    def twin_id(pair):
        return {
            "grp": other + pair // per_group,
            "tp": lax.rem(pair, per_group) * CORES + core,
        }

    sibling = {"tp": place * CORES + 1 - core}

    def slot_copies(i, s):
        start = pl.multiple_of(i * chunk, chunk)
        return (
            pltpu.make_async_copy(
                gate_hbm.at[0, pl.ds(start, chunk), :], slots.at[s, 0], slot_sem.at[s]
            ),
            pltpu.make_async_copy(
                up_hbm.at[0, pl.ds(start, chunk), :], slots.at[s, 1], slot_sem.at[s]
            ),
        )

    def down_copy(c, s):
        start = pl.multiple_of(c * down_cols, down_cols)
        return pltpu.make_async_copy(
            down_hbm.at[0, :, pl.ds(start, down_cols)], down_slots.at[s], down_sem.at[s]
        )

    small_copies = (
        pltpu.make_async_copy(queries_hbm, queries, small_sem.at[0]),
        pltpu.make_async_copy(fresh_keys_hbm, fresh_keys, small_sem.at[1]),
        pltpu.make_async_copy(fresh_values_hbm, fresh_values, small_sem.at[2]),
        pltpu.make_async_copy(residual_hbm, residual, small_sem.at[3]),
        pltpu.make_async_copy(gain_hbm, gain, small_sem.at[4]),
    )
    key_copy = pltpu.make_async_copy(key_hbm.at[0, 0], keys, cache_sem.at[0])
    value_copy = pltpu.make_async_copy(value_hbm.at[0, 0], values, cache_sem.at[1])

    @pl.when(serving)
    def _():
        small_copies[0].start()
        key_copy.start()
        for copy in small_copies[1:]:
            copy.start()
        value_copy.start()

    @pl.when(jnp.logical_not(serving))
    def _():
        for i in range(ring):
            for copy in slot_copies(i, i):
                copy.start()
        for c in range(down_ring):
            down_copy(c, c).start()

    @pl.loop(0, pairs)
    def _(i):
        pl.semaphore_signal(barrier, inc=1, device_id=twin_id(i), device_id_type=MESH_ID)

    @pl.when(serving)
    def _():
        slot_count = keys.shape[0]
        scale = HD ** (-0.5)
        usable = lax.broadcasted_iota(jnp.int32, (SHARE, slot_count), 1) < lengths[0, 0]
        for copy in small_copies:
            copy.wait()
        key_copy.wait()
        value_copy.wait()
        query = queries[0, 0].astype(f32).reshape(HEADS, HD)
        stream = residual[0, 0].astype(f32).reshape(HEADS, HD)
        own_key = fresh_keys[0, 0].astype(f32).reshape(KVH, HD)
        own_value = fresh_values[0, 0].astype(f32).reshape(KVH, HD)
        spread = jnp.zeros((1, 1), f32)
        for j in range(KVH):
            head = slice(j * SHARE, (j + 1) * SHARE)
            lanes = slice(j * HD, (j + 1) * HD)
            own = query[head, :]
            scores = (
                lax.dot_general(
                    own.astype(bf16), keys[:, lanes], NT, preferred_element_type=f32
                )
                * scale
            )
            scores = jnp.where(usable, scores, masked_score)
            fresh = jnp.sum(own * own_key[j : j + 1, :], axis=-1, keepdims=True) * scale
            ceiling = jnp.maximum(jnp.max(scores, axis=-1, keepdims=True), fresh)
            expo = jnp.where(usable, jnp.exp(scores - ceiling), 0.0)
            fresh_expo = jnp.exp(fresh - ceiling)
            denominator = jnp.sum(expo, axis=-1, keepdims=True) + fresh_expo
            total = jnp.dot(expo.astype(bf16), values[:, lanes], preferred_element_type=f32)
            total = total + fresh_expo.astype(bf16).astype(f32) * own_value[j : j + 1, :]
            row = stream[head, :] + total / denominator
            hidden[head, :] = row
            squares = jnp.sum(row * row, axis=-1, keepdims=True)
            spread = spread + jnp.sum(squares, axis=0, keepdims=True)
        factor = lax.rsqrt(spread / (HEADS * HD) + 1e-05)
        normed[...] = (hidden[...] * factor * gain[...]).astype(bf16)
        pl.semaphore_wait(barrier, pairs)
        row = core * pairs + mine

        @pl.loop(0, pairs)
        def _(i):
            pltpu.make_async_remote_copy(
                src_ref=normed,
                dst_ref=box.at[row],
                send_sem=row_send,
                recv_sem=row_recv.at[row],
                device_id=twin_id(pair_at(i)),
                device_id_type=MESH_ID,
            ).start()

        sent = box.at[pl.ds(0, pairs)]
        pltpu.make_async_copy(sent, sent, row_send).wait()

        for b in range(batches):
            band = slice(b * batch, (b + 1) * batch)
            got = back.at[:, band, :]
            pltpu.make_async_copy(got, got, back_recv.at[b]).wait()
            total = hidden[band, :]
            total = lax.fori_loop(
                0, pairs, lambda p, so_far: so_far + back[p, band, :].astype(f32), total
            )
            out[0, 0, :, b * batch * HD : (b + 1) * batch * HD] = total.reshape(
                1, batch * HD
            ).astype(bf16)

    @pl.when(jnp.logical_not(serving))
    def _():
        out[...] = jnp.zeros_like(out)
        pl.semaphore_signal(barrier, inc=1, device_id=sibling, device_id_type=MESH_ID)
        pl.semaphore_wait(barrier, pairs + 1)

        def widen(row):
            start = pl.multiple_of(row * STRIDE, 8)
            wide[pl.ds(start, HEADS), :] = box[row].astype(f32)

        def arrived(row):
            here = box.at[row]
            pltpu.make_async_copy(here, here, row_recv.at[row]).wait()

        @pl.loop(0, pairs)
        def _(i):
            row = core * pairs + pair_at(i)
            arrived(row)
            pltpu.make_async_remote_copy(
                src_ref=box.at[row],
                dst_ref=box.at[row],
                send_sem=pass_send,
                recv_sem=row_recv.at[row],
                device_id=sibling,
                device_id_type=MESH_ID,
            ).start()
            widen(row)

        @pl.loop(0, pairs)
        def _(i):
            row = (1 - core) * pairs + pair_at(i)
            arrived(row)
            widen(row)

        for h in range(HEADS):
            rows[:, h * HD : (h + 1) * HD] = wide[pl.ds(h, peers, stride=STRIDE), :].astype(bf16)

        sent = box.at[pl.ds(0, pairs)]
        pltpu.make_async_copy(sent, sent, pass_send).wait()

        def hidden_units(start, count):
            at = [lax.rem(start + k, ring) for k in range(count)]
            for s in at:
                pltpu.make_async_copy(slots.at[s], slots.at[s], slot_sem.at[s]).wait()
            for k, s in enumerate(at):
                spot = pl.ds(pl.multiple_of((start + k) * chunk, chunk), chunk)
                if chunks == 1:
                    spot = slice(None)
                for which, store in enumerate((gate_out, up_out)):
                    store[:, spot] = lax.dot_general(
                        rows[...], slots[s, which], NT, preferred_element_type=f32
                    )
            for k, s in enumerate(at):

                @pl.when(start + k + ring < chunks)
                def _():
                    for copy in slot_copies(start + k + ring, s):
                        copy.start()

        step = 2

        @pl.loop(0, chunks // step)
        def _(i):
            hidden_units(i * step, step)

        if chunks % step:
            hidden_units(chunks - chunks % step, chunks % step)

        gate = gate_out[...]
        act[...] = (gate / (1.0 + jnp.exp(-gate)) * up_out[...]).astype(bf16)

        def send_back(g):
            base = pl.multiple_of(g * batch, batch)
            cols = pl.ds(pl.multiple_of(g * batch * HD, batch * HD), batch * HD)
            got = cross_in.at[:, cols]
            pltpu.make_async_copy(got, got, cross_recv.at[g]).wait()
            total = keep[:, cols] + cross_in[:, cols]
            for h in range(batch):
                wide[pl.ds(h, pairs, stride=STRIDE), :] = total[:, h * HD : (h + 1) * HD]
            for r in range(pairs):
                part[r, pl.ds(base, batch), :] = wide[
                    r * STRIDE : r * STRIDE + batch, :
                ].astype(bf16)

            @pl.loop(0, pairs)
            def _(i):
                to = pair_at(i)
                pltpu.make_async_remote_copy(
                    src_ref=part.at[to, pl.ds(base, batch), :],
                    dst_ref=back.at[mine, pl.ds(base, batch), :],
                    send_sem=back_send,
                    recv_sem=back_recv.at[g],
                    device_id=twin_id(to),
                    device_id_type=MESH_ID,
                ).start()

        @pl.loop(0, batches)
        def _(g):
            for k in range(per_batch):
                c = g * per_batch + k
                s = lax.rem(c, down_ring)
                cols = pl.ds(pl.multiple_of(c * down_cols, down_cols), down_cols)
                pltpu.make_async_copy(down_slots.at[s], down_slots.at[s], down_sem.at[s]).wait()
                feed = jnp.dot(act[...], down_slots[s], preferred_element_type=f32)

                @pl.when(c + down_ring < down_chunks)
                def _():
                    down_copy(c + down_ring, s).start()

                low, high = feed[:pairs, :], feed[pairs:, :]
                keep[:, cols] = jnp.where(core == 0, low, high)
                cross_out[:, cols] = jnp.where(core == 0, high, low)

            cols = pl.ds(pl.multiple_of(g * batch * HD, batch * HD), batch * HD)
            pltpu.make_async_remote_copy(
                src_ref=cross_out.at[:, cols],
                dst_ref=cross_in.at[:, cols],
                send_sem=cross_send,
                recv_sem=cross_recv.at[g],
                device_id=sibling,
                device_id_type=MESH_ID,
            ).start()

            @pl.when(g > 0)
            def _():
                send_back(g - 1)

        send_back(batches - 1)
        pltpu.make_async_copy(cross_out, cross_out, cross_send).wait()
        pltpu.make_async_copy(part, part, back_send).wait()


def local(
    key_cache,
    value_cache,
    lengths,
    queries,
    new_keys,
    new_values,
    residual,
    norm_gain,
    gate_weight,
    up_weight,
    down_weight,
):
    groups = lax.axis_size("grp")
    members = lax.axis_size("tp")
    half = groups // 2
    peers = half * members
    pairs = peers // CORES
    width = queries.shape[3]
    slot_count = key_cache.shape[2]
    units = gate_weight.shape[1]
    chunk = HD if units % HD == 0 else units
    chunks = units // chunk
    slot_bytes = 4 * chunk * width
    ring = max(1, min(chunks, 42_000_000 // slot_bytes))
    down_cols = 512
    down_chunks = width // down_cols
    down_ring = min(down_chunks, max(1, 20_500_000 // (2 * units * down_cols)))
    batch = 16
    batches = HEADS // batch
    plan = (half, members, chunk, chunks, ring, down_cols, down_chunks, down_ring, batch)
    vmem = pl.BlockSpec(memory_space=pltpu.VMEM)
    any_space = pl.BlockSpec(memory_space=pl.ANY)
    dma = pltpu.SemaphoreType.DMA
    return pl.pallas_call(
        functools.partial(kernel, plan),
        out_shape=jax.ShapeDtypeStruct(queries.shape, bf16),
        in_specs=[pl.BlockSpec(memory_space=pltpu.SMEM)] + [any_space] * 10,
        out_specs=vmem,
        scratch_shapes=[
            pltpu.VMEM((slot_count, KVH * HD), bf16),
            pltpu.VMEM((slot_count, KVH * HD), bf16),
            pltpu.VMEM(queries.shape, bf16),
            pltpu.VMEM(new_keys.shape, bf16),
            pltpu.VMEM(new_values.shape, bf16),
            pltpu.VMEM(residual.shape, bf16),
            pltpu.VMEM((HEADS, HD), f32),
            pltpu.VMEM((HEADS, HD), f32),
            pltpu.VMEM((HEADS, HD), bf16),
            pltpu.VMEM((peers, HEADS, HD), bf16),
            pltpu.VMEM((peers * STRIDE, HD), f32),
            pltpu.VMEM((peers, width), bf16),
            pltpu.VMEM((peers, units), f32),
            pltpu.VMEM((peers, units), f32),
            pltpu.VMEM((peers, units), bf16),
            pltpu.VMEM((pairs, width), f32),
            pltpu.VMEM((pairs, width), f32),
            pltpu.VMEM((pairs, width), f32),
            pltpu.VMEM((pairs, HEADS, HD), bf16),
            pltpu.VMEM((pairs, HEADS, HD), bf16),
            pltpu.VMEM((ring, 2, chunk, width), bf16),
            pltpu.VMEM((down_ring, units, down_cols), bf16),
            dma((2,)),
            dma((5,)),
            dma((ring,)),
            dma((down_ring,)),
            dma,
            dma((peers,)),
            dma,
            dma,
            dma((batches,)),
            dma,
            dma((batches,)),
        ],
        compiler_params=pltpu.CompilerParams(
            collective_id=0, has_side_effects=True, vmem_limit_bytes=VMEM_BYTES
        ),
    )(
        lengths,
        norm_gain.reshape(HEADS, HD),
        queries,
        new_keys,
        new_values,
        residual,
        key_cache,
        value_cache,
        gate_weight,
        up_weight,
        down_weight,
    )


def solution(mesh):
    return jax.shard_map(
        local,
        mesh=mesh,
        in_specs=(
            P("grp", "tp", None, None),
            P("grp", "tp", None, None),
            P("grp", "tp"),
            P("grp", None, "tp", None),
            P("grp", None, "tp", None),
            P("grp", None, "tp", None),
            P("grp", None, "tp", None),
            P(),
            P("grp", "tp", None),
            P("grp", "tp", None),
            P("grp", "tp", None),
        ),
        out_specs=P("grp", None, "tp", None),
        check_vma=False,
    )
```

time: 53 us -> 43.8 us (0.83)
  other arithmetic: 5.43 us -> 0 us
  Pallas kernels: 45.1 us -> 41.5 us
    unnamed x4 -> x0, other arithmetic: 5.43 us -> none
    pallas_call x1, Pallas kernels: 45.1 us -> 41.5 us  [local(): pl.pallas_call(functools.partial(kernel, plan), out_shape=jax.ShapeDtypeS...]
    unnamed x0 -> x1, local copies, waits for them, and re-layouts: none -> 1.41 us
    reshape x1 -> x0, local copies, waits for them, and re-layouts: 1.34 us -> none  [local(): return mixed.reshape(1, 1, 1, width)]
where the time goes in v1:
time: 43.8 us; the launch traced here: 43.6 us
  Pallas kernels  41.5 us (95%)
  local copies, waits for them, and re-layouts  1.41 us (3%)
  between operations  0.66 us (2%)
    pallas_call x1, Pallas kernels, local(): pl.pallas_call(functools.partial(kernel, plan), out_shape=jax.ShapeDtypeS...  41.5 us
    unnamed x1, local copies, waits for them, and re-layouts  1.41 us

profile of v1, /device:TPU:0, one launch (start us, length us, event | category | flops | bytes accessed | tf_op | source)
XLA Modules:
  0.0 43.6 jit_solution(13555574904727386509)
XLA Ops:
  0.7 41.5 %shard_map.109 = bf16[1,1,1,8192]{3,2,1,0:T(2,128)(2,1)} custom-call(s32[1,1]{1,0:T(1,128)S(6)} %copy.13.lengths, f32[64,128]{1,0:T(8,128)} %bitcast.1, bf16[1,1,1,8192]{3,2,1,0:T(2,128)(2,1)} %queries_hbm.1, bf16[1,1,1,512]{3,2,1,0:T(2,128)(2,1)} %fresh_keys_hbm.1, bf16[1,1,1,512]{3,2,1,0:T(2,128)(2,1)} %fresh_values_hbm.1, ...), custom_call_target="tpu_custom_call" | custom-call | tf_op jit(solution)/shard_map/pallas_call | solution.py:384
  42.1 1.4 %copy.14 = bf16[1,1,1,8192]{3,2,1,0:T(2,128)(2,1)} copy(bf16[1,1,1,8192]{3,2,1,0:T(2,128)(2,1)} %shard_map.109) | data formatting | bytes 32768
